TPU v7x, 32 devices: a whole 2x2x4 slice. The times are simulated.
32 devices in a mesh: dom: 8 (over z, y), edge: 4 (over x, core).
Axes of the slice: x: 2, y: 2, z: 4, core: 2. Of those that a mesh axis runs over, the one named last changes fastest.
Arguments:
- fine_nodes: bfloat16 [65536, 128], P('dom'), may hold values from -6 to 6
- fine_edges: bfloat16 [131072, 128], P(('dom', 'edge')), may hold values from -6 to 6
- fine_senders: int32 [131072], P(('dom', 'edge')), may hold values from 0 to 8703, as said below
- fine_receivers: int32 [131072], P(('dom', 'edge')), may hold values from 0 to 8191
- fine_halo: int32 [8, 8, 64], P('dom'), may hold values from 0 to 8191
- coarse_edges: bfloat16 [32768, 128], P(('dom', 'edge')), may hold values from -6 to 6
- coarse_senders: int32 [32768], P(('dom', 'edge')), may hold values from 0 to 2303, as said below
- coarse_receivers: int32 [32768], P(('dom', 'edge')), may hold values from 0 to 2047
- coarse_halo: int32 [8, 8, 32], P('dom'), may hold values from 0 to 2047
- pool_send: int32 [8, 8, 1536], P('dom'), may hold values from 0 to 8191, as said below
- pool_dest: int32 [8, 8, 1536], P('dom'), may hold values from 0 to 2048, as said below
- unpool_slot: int32 [65536], P('dom'), may hold values from 0 to 12287, as said below
- edge_in_weight: bfloat16 [2, 384, 128], replicated, may hold values from -0.3125 to 0.3125
- edge_out_weight: bfloat16 [2, 128, 128], replicated, may hold values from -0.5 to 0.5
- node_in_weight: bfloat16 [2, 256, 128], replicated, may hold values from -0.375 to 0.375
- node_out_weight: bfloat16 [2, 128, 128], replicated, may hold values from -0.5 to 0.5
- edge_gain: float32 [2, 128], replicated, may hold values from 0.5 to 1.5
- node_gain: float32 [2, 128], replicated, may hold values from 0.5 to 1.5
Outputs:
- fine_out: bfloat16 [65536, 128], P('dom')
- coarse_out: bfloat16 [16384, 128], P('dom')
Inputs may be any that keep to these rules, and one draw needn't show every extreme that they name: `fine_senders`: an entry below 8192 is a row of the edge's own partition; an entry 8192 + d * 64 + s names slot s of fine_halo[d, p] for the edge's partition p. `coarse_senders`: an entry below 2048 is a row of the edge's own coarse partition; an entry 2048 + d * 32 + s names slot s of coarse_halo[d, p]. pool_send[d, p, s] is a row of partition d. For each pair (d, p) the slots that carry data come first and number at most 1536; in every draw some p receives 1536 from every d. Every row of partition d is carried exactly once over all p and s; empty slots hold 0. pool_dest[p, d, s] is 2048 exactly where slot s of pool_send[d, p] is empty, else a row of coarse partition p. `unpool_slot`: row r of partition d holds p * 1536 + s for the one carrying slot with pool_send[d, p, s] = r.
All inputs are finite; a program needn't handle non-finite values.
Results may differ from a plain program's by a relative error of at most 0.0068.
Values may be sent and summed in bfloat16 or wider, within the bound.
No kernel may reach another device: no remote copies, remote signals or barrier semaphores. Data moves between devices by JAX's collectives and lax.ppermute only.
A program may use at most 64 MiB of HBM per device.

v0:
```python
import jax
import jax.numpy as jnp
from jax import lax
from jax.sharding import PartitionSpec as P

COARSE = 2048


def layer_norm(values, gain):
    center = values - jnp.mean(values, axis=-1, keepdims=True)
    spread = jnp.mean(center * center, axis=-1, keepdims=True)
    return center * lax.rsqrt(spread + 1e-05) * gain


def node_update(rows, summed, w_first, w_second, gain):
    inputs = jnp.concatenate([rows, summed.astype(jnp.bfloat16)], axis=1)
    hidden = jax.nn.silu(jnp.dot(inputs, w_first, preferred_element_type=jnp.float32)).astype(
        jnp.bfloat16
    )
    result = layer_norm(jnp.dot(hidden, w_second, preferred_element_type=jnp.float32), gain)
    return (rows.astype(jnp.float32) + result).astype(jnp.bfloat16)


def graph_layer(nodes, edges, senders, receivers, border, level, weights):
    edge_in_weight, edge_out_weight, node_in_weight, node_out_weight, edge_gain, node_gain = weights
    width = nodes.shape[-1]
    outgoing = nodes[border[0]]
    ghosts = lax.all_to_all(outgoing, "dom", split_axis=0, concat_axis=0, tiled=True)
    table = jnp.concatenate([nodes, ghosts.reshape(-1, width)], axis=0)
    inputs = jnp.concatenate([table[senders], nodes[receivers], edges], axis=1)
    hidden = jax.nn.silu(
        jnp.dot(inputs, edge_in_weight[level], preferred_element_type=jnp.float32)
    ).astype(jnp.bfloat16)
    message = layer_norm(
        jnp.dot(hidden, edge_out_weight[level], preferred_element_type=jnp.float32),
        edge_gain[level],
    )
    partial_sum = jax.ops.segment_sum(message, receivers, num_segments=nodes.shape[0])
    summed = lax.psum(partial_sum, "edge")
    return node_update(
        nodes, summed, node_in_weight[level], node_out_weight[level], node_gain[level]
    )


def pooled_mean(arrived, places, width):
    sums = jax.ops.segment_sum(
        arrived.reshape(-1, width).astype(jnp.float32), places, num_segments=COARSE + 1
    )[:COARSE]
    counts = jax.ops.segment_sum(jnp.ones_like(places), places, num_segments=COARSE + 1)[:COARSE]
    return (sums / jnp.maximum(counts, 1).astype(jnp.float32)[:, None]).astype(jnp.bfloat16)


def shards(
    fine_nodes,
    fine_edges,
    fine_senders,
    fine_receivers,
    fine_halo,
    coarse_edges,
    coarse_senders,
    coarse_receivers,
    coarse_halo,
    pool_send,
    pool_dest,
    unpool_slot,
    edge_in_weight,
    edge_out_weight,
    node_in_weight,
    node_out_weight,
    edge_gain,
    node_gain,
):
    weights = (
        edge_in_weight,
        edge_out_weight,
        node_in_weight,
        node_out_weight,
        edge_gain,
        node_gain,
    )
    width = fine_nodes.shape[-1]
    fine_mid = graph_layer(
        fine_nodes, fine_edges, fine_senders, fine_receivers, fine_halo, 0, weights
    )
    places = pool_dest[0].reshape(-1)
    arrived = lax.all_to_all(fine_mid[pool_send[0]], "dom", split_axis=0, concat_axis=0, tiled=True)
    coarse_in = pooled_mean(arrived, places, width)
    coarse_out = graph_layer(
        coarse_in, coarse_edges, coarse_senders, coarse_receivers, coarse_halo, 1, weights
    )
    padded = jnp.concatenate([coarse_out, jnp.zeros((1, width), jnp.bfloat16)], axis=0)
    back = lax.all_to_all(padded[pool_dest[0]], "dom", split_axis=0, concat_axis=0, tiled=True)
    parents = back.reshape(-1, width)[unpool_slot]
    fine_out = (fine_mid.astype(jnp.float32) + parents.astype(jnp.float32)).astype(jnp.bfloat16)
    return (fine_out, coarse_out)


def solution(mesh):
    placed = (
        P("dom", None),
        P(("dom", "edge"), None),
        P(("dom", "edge")),
        P(("dom", "edge")),
        P("dom", None, None),
        P(("dom", "edge"), None),
        P(("dom", "edge")),
        P(("dom", "edge")),
        P("dom", None, None),
        P("dom", None, None),
        P("dom", None, None),
        P("dom"),
        P(),
        P(),
        P(),
        P(),
        P(),
        P(),
    )
    return jax.shard_map(
        shards,
        mesh=mesh,
        in_specs=placed,
        out_specs=(P("dom", None), P("dom", None)),
        check_vma=False,
    )
```

profile of v0, /device:TPU:0, one launch (start us, length us, event | category | flops | bytes accessed | tf_op | source)
XLA Modules:
  0.0 604.5 jit_solution(17450261135767377777)
XLA Ops:
  0.6 0.7 compare_select_fusion.8
  1.3 0.1 reshape.183
  1.4 3.5 gather_fusion
  4.9 7.3 %all-to-all-start = ((bf16[8,64,128]{2,1,0:T(8,128)(2,1)}), bf16[8,64,128]{2,1,0:T(8,128)(2,1)S(1)}, u32[]{:S(2)}, u32[]{:S(2)}) async-start(bf16[8,64,128]{2,1,0:T(8,128)(2,1)} %bitcast.1), calls=%async_computation | async-start | bytes 262144 | tf_op jit(solution)/shard_map/all_to_all | solution.py:28
  12.2 0.7 fusion.77
  13.0 0.8 slice_bitcast_fusion.1
  13.7 1.0 compare_select_fusion.1
  14.7 0.8 slice_bitcast_fusion
  15.5 4.1 copy.24
  19.5 12.1 %gather_fusion.2 = bf16[4096,128]{1,0:T(8,128)(2,1)S(1)} fusion(bf16[8192,128]{1,0:T(8,128)(2,1)S(1)} %copy-done, s32[4096]{0:T(1024)S(1)} %fusion.77), kind=kCustom, calls=%fused_computation.2 | custom fusion | bytes 2113536 | tf_op jit(solution)/shard_map/gather | solution.py:30
  31.7 0.0 copy-done.8
  31.7 0.0 all-to-all-done
  31.7 5.6 pad_maximum_fusion
  37.3 16.2 %gather_fusion.1 = bf16[4096,128]{1,0:T(8,128)(2,1)} fusion(bf16[8704,128]{1,0:T(8,128)(2,1)} %pad_maximum_fusion, s32[4096]{0:T(1024)S(1)} %fusion.76), kind=kCustom, calls=%fused_computation.1 | custom fusion | bytes 2113536 | tf_op jit(solution)/shard_map/gather | solution.py:30
  53.5 0.0 copy-done.15
  53.5 4.3 fusion.95
  57.8 2.0 multiply_reduce_fusion.1
  59.8 0.2 copy-done.4
  60.0 1.7 multiply_multiply_fusion
  61.7 2.9 copy.25
  64.6 24.8 %scatter_custom_fusion = f32[8192,128]{1,0:T(8,128)} fusion(s32[4096]{0:T(1024)} %param.21, f32[4096,128]{1,0:T(8,128)} %copy.25, f32[]{:T(128)} %constant.13.clone.1), kind=kCustom, calls=%fused_computation.33 | custom fusion | flops 524288 | bytes 4194816 | tf_op jit(solution)/shard_map/scatter-add | solution.py:38
  89.4 77.1 %all-reduce.3 = bf16[8192,128]{1,0:T(8,128)(2,1)} all-reduce(f32[8192,128]{1,0:T(8,128)} %scatter_custom_fusion), channel_id=1, replica_groups=mesh['dom'=8,'edge'=4] {'edge'}, use_global_device_ids=true, to_apply=%region_3.4 | all-reduce | flops 1048576 | bytes 6291456 | tf_op jit(solution)/shard_map/psum | solution.py:39
  166.5 0.0 copy-done.14
  166.5 5.8 fusion.100
  172.3 2.8 multiply_reduce_fusion
  175.1 0.6 copy-done.2
  175.7 3.8 add_convert_fusion.1
  179.5 3.2 copy.26
  182.7 43.3 %gather_fusion.3 = bf16[12288,128]{1,0:T(8,128)(2,1)} fusion(bf16[8192,128]{1,0:T(8,128)(2,1)S(1)} %copy.26, s32[12288]{0:T(1024)S(1)} %broadcast_clamp_fusion.1), kind=kCustom, calls=%fused_computation.3 | custom fusion | bytes 6340608 | tf_op jit(solution)/shard_map/gather | solution.py:86
  226.0 5.5 all-to-all-start.1
  231.6 0.0 copy-done.6
  231.6 0.1 reshape.215
  231.7 75.2 %scatter_custom_fusion.2 = s32[2049]{0:T(1024)S(1)} fusion(s32[12288]{0:T(1024)S(1)} %reshape.263, s32[12288]{0:T(1024)S(1)} %broadcast.163, s32[]{:T(128)} %constant.14.clone.1), kind=kCustom, calls=%fused_computation.101 | custom fusion | flops 12288 | bytes 8200 | tf_op jit(solution)/shard_map/scatter-add | solution.py:49
  307.0 0.0 all-to-all-done.1
  307.0 0.0 copy-start.11
  307.1 76.8 %scatter_custom_fusion.1 = f32[2049,128]{1,0:T(8,128)} fusion(s32[12288]{0:T(1024)S(1)} %reshape.263, bf16[12288,128]{1,0:T(8,128)(2,1)S(1)} %bitcast.78, f32[]{:T(128)} %constant.13.clone.1), kind=kCustom, calls=%fused_computation.13 | custom fusion | flops 3145728 | bytes 4194820 | tf_op jit(solution)/shard_map/scatter-add | solution.py:46
  383.8 1.6 fusion.24
  385.4 1.5 gather_fusion.4
  386.8 11.6 %all-to-all-start.2 = ((bf16[8,32,128]{2,1,0:T(8,128)(2,1)}), bf16[8,32,128]{2,1,0:T(8,128)(2,1)S(1)}, u32[]{:S(2)}, u32[]{:S(2)}) async-start(bf16[8,32,128]{2,1,0:T(8,128)(2,1)} %bitcast.13), calls=%async_computation.2 | async-start | bytes 131072 | tf_op jit(solution)/shard_map/all_to_all | solution.py:28
  398.5 3.2 gather_fusion.6
  401.7 0.0 copy-start.12
  401.7 0.0 copy-start.13
  401.7 0.0 copy-start.16
  401.8 3.6 all-to-all-done.2
  405.4 3.2 gather_fusion.5
  408.7 0.6 fusion.105
  409.3 0.1 multiply_reduce_fusion.3
  409.4 0.1 multiply_multiply_fusion.1
  409.5 0.0 copy-start.18
  409.5 0.2 copy.27
  409.7 6.3 %scatter_custom_fusion.3 = f32[2048,128]{1,0:T(8,128)S(1)} fusion(s32[1024]{0:T(1024)S(1)} %copy-done.11, f32[1024,128]{1,0:T(8,128)S(1)} %copy.27, f32[]{:T(128)} %constant.13.clone.1), kind=kCustom, calls=%fused_computation.61 | custom fusion | flops 131072 | bytes 1048580 | tf_op jit(solution)/shard_map/scatter-add | solution.py:38
  416.0 25.8 %all-reduce.4 = bf16[2048,128]{1,0:T(8,128)(2,1)S(1)} all-reduce(f32[2048,128]{1,0:T(8,128)S(1)} %scatter_custom_fusion.3), channel_id=1, replica_groups=mesh['dom'=8,'edge'=4] {'edge'}, use_global_device_ids=true, to_apply=%region_11.12 | all-reduce | flops 262144 | bytes 1572864 | tf_op jit(solution)/shard_map/psum | solution.py:39
  441.8 0.9 fusion.110
  442.7 0.6 multiply_reduce_fusion.2
  443.3 1.0 add_convert_fusion.2
  444.3 0.0 copy-start.5
  444.3 0.8 copy-done.5
  445.2 43.3 %gather_fusion.7 = bf16[12288,128]{1,0:T(8,128)(2,1)} fusion(bf16[2049,128]{1,0:T(8,128)(2,1)S(1)} %concatenate.27, s32[12288]{0:T(1024)S(1)} %broadcast_clamp_fusion), kind=kCustom, calls=%fused_computation.7 | custom fusion | bytes 6340608 | tf_op jit(solution)/shard_map/gather | solution.py:92
  488.5 3.8 all-to-all-start.3
  492.3 71.3 %all-to-all-done.3 = bf16[8,1536,128]{2,1,0:T(8,128)(2,1)S(1)} async-done(((bf16[8,1536,128]{2,1,0:T(8,128)(2,1)}), bf16[8,1536,128]{2,1,0:T(8,128)(2,1)S(1)}, u32[]{:S(2)}, u32[]{:S(2)}) %all-to-all-start.3) | async-done | bytes 3145760 | tf_op jit(solution)/shard_map/all_to_all | solution.py:92
  563.6 29.2 %gather_fusion.8 = bf16[8192,128]{1,0:T(8,128)(2,1)} fusion(bf16[12288,128]{1,0:T(8,128)(2,1)S(1)} %bitcast.77, s32[8192]{0:T(1024)S(1)} %fusion.67), kind=kCustom, calls=%fused_computation.8 | custom fusion | bytes 4227072 | tf_op jit(solution)/shard_map/gather | solution.py:93
  592.8 4.2 copy.28
  597.1 3.4 add_convert_fusion
  600.5 4.1 copy.29
  (50 shorter events, 0.3 us)
Async XLA Ops:
  4.9 26.8 %all-to-all-start = ((bf16[8,64,128]{2,1,0:T(8,128)(2,1)}), bf16[8,64,128]{2,1,0:T(8,128)(2,1)S(1)}, u32[]{:S(2)}, u32[]{:S(2)}) async-start(bf16[8,64,128]{2,1,0:T(8,128)(2,1)} %bitcast.1), calls=%async_computation | async-start | bytes 262144 | tf_op jit(solution)/shard_map/all_to_all | solution.py:28
  13.7 5.8 copy-start
  19.5 12.1 %copy-start.8 = (s32[4096]{0:T(1024)S(1)}, s32[4096]{0:T(1024)}, u32[]{:S(2)}) copy-start(s32[4096]{0:T(1024)} %param.20) | copy-start | bytes 49156
  37.3 16.2 %copy-start.15 = (bf16[2,128,128]{2,1,0:T(8,128)(2,1)S(1)}, bf16[2,128,128]{2,1,0:T(8,128)(2,1)}, u32[]{:S(2)}) copy-start(bf16[2,128,128]{2,1,0:T(8,128)(2,1)} %param.31) | copy-start | bytes 196612
  57.8 2.2 copy-start.4
  89.4 77.1 %copy-start.14 = (bf16[2,256,128]{2,1,0:T(8,128)(2,1)S(1)}, bf16[2,256,128]{2,1,0:T(8,128)(2,1)}, u32[]{:S(2)}) copy-start(bf16[2,256,128]{2,1,0:T(8,128)(2,1)} %param.32) | copy-start | bytes 393220
  89.4 77.1 %copy-start.17 = (bf16[2,128,128]{2,1,0:T(8,128)(2,1)S(1)}, bf16[2,128,128]{2,1,0:T(8,128)(2,1)}, u32[]{:S(2)}) copy-start(bf16[2,128,128]{2,1,0:T(8,128)(2,1)} %param.33) | copy-start | bytes 196612
  172.3 3.4 copy-start.2
  226.0 5.5 copy-start.6
  226.0 5.5 copy-start.9
  226.0 81.0 %copy-start.10 = (s32[1024]{0:T(1024)S(1)}, s32[1024]{0:T(1024)}, u32[]{:S(2)}) copy-start(s32[1024]{0:T(1024)} %param.24) | copy-start | bytes 12292
  226.0 81.0 %all-to-all-start.1 = ((bf16[8,1536,128]{2,1,0:T(8,128)(2,1)}), bf16[8,1536,128]{2,1,0:T(8,128)(2,1)S(1)}, u32[]{:S(2)}, u32[]{:S(2)}) async-start(bf16[8,1536,128]{2,1,0:T(8,128)(2,1)} %bitcast.79), calls=%async_computation.1 | async-start | bytes 6291456 | tf_op jit(solution)/shard_map/all_to_all | solution.py:86
  307.0 91.4 %copy-start.11 = (s32[1024]{0:T(1024)S(1)}, s32[1024]{0:T(1024)}, u32[]{:S(2)}) copy-start(s32[1024]{0:T(1024)} %param.25) | copy-start | bytes 12292
  386.8 18.5 %all-to-all-start.2 = ((bf16[8,32,128]{2,1,0:T(8,128)(2,1)}), bf16[8,32,128]{2,1,0:T(8,128)(2,1)S(1)}, u32[]{:S(2)}, u32[]{:S(2)}) async-start(bf16[8,32,128]{2,1,0:T(8,128)(2,1)} %bitcast.13), calls=%async_computation.2 | async-start | bytes 131072 | tf_op jit(solution)/shard_map/all_to_all | solution.py:28
  401.7 6.9 %copy-start.12 = (bf16[1024,128]{1,0:T(8,128)(2,1)S(1)}, bf16[1024,128]{1,0:T(8,128)(2,1)}, u32[]{:S(2)}) copy-start(bf16[1024,128]{1,0:T(8,128)(2,1)} %param.23) | copy-start | bytes 786436
  401.7 6.9 %copy-start.13 = (bf16[2,384,128]{2,1,0:T(8,128)(2,1)S(1)}, bf16[2,384,128]{2,1,0:T(8,128)(2,1)}, u32[]{:S(2)}) copy-start(bf16[2,384,128]{2,1,0:T(8,128)(2,1)} %param.30) | copy-start | bytes 589828
  401.7 6.9 %copy-start.16 = (bf16[2,128,128]{2,1,0:T(8,128)(2,1)S(1)}, bf16[2,128,128]{2,1,0:T(8,128)(2,1)}, u32[]{:S(2)}) copy-start(bf16[2,128,128]{2,1,0:T(8,128)(2,1)} %param.31) | copy-start | bytes 196612
  409.5 32.3 %copy-start.18 = (bf16[2,128,128]{2,1,0:T(8,128)(2,1)S(1)}, bf16[2,128,128]{2,1,0:T(8,128)(2,1)}, u32[]{:S(2)}) copy-start(bf16[2,128,128]{2,1,0:T(8,128)(2,1)} %param.33) | copy-start | bytes 196612
  441.8 1.5 copy-start.3
  444.3 0.8 copy-start.5
  488.5 3.8 copy-start.7
  488.5 75.1 %all-to-all-start.3 = ((bf16[8,1536,128]{2,1,0:T(8,128)(2,1)}), bf16[8,1536,128]{2,1,0:T(8,128)(2,1)S(1)}, u32[]{:S(2)}, u32[]{:S(2)}) async-start(bf16[8,1536,128]{2,1,0:T(8,128)(2,1)} %bitcast.80), calls=%async_computation.3 | async-start | bytes 6291456 | tf_op jit(solution)/shard_map/all_to_all | solution.py:92
  592.8 4.2 copy-start.1
where the time goes:
time: 606 us; the launch traced here: 605 us
  other arithmetic  208 us (34%)
  local copies, waits for them, and re-layouts  178 us (29%)
  blocking collectives  103 us (17%)
  waiting for transfers between devices  74.9 us (12%)
  starting transfers between devices  28.2 us (5%)
  matrix products  11.6 us (2%)
    psum x2, blocking collectives, graph_layer(): summed = lax.psum(partial_sum, 'edge')  103 us
    scatter-add x1, other arithmetic, pooled_mean(): jax.ops.segment_sum(arrived.reshape(-1, width).astype(jnp.float32), place...  76.8 us
    scatter-add x1, other arithmetic, pooled_mean(): jax.ops.segment_sum(jnp.ones_like(places), places, num_segments=COARSE + 1)  75.2 us
    all_to_all x1, waiting for transfers between devices, shards(): lax.all_to_all(padded[pool_dest[0]], 'dom', split_axis=0, concat_axis=0,...  71.3 us
    gather x1, local copies, waits for them, and re-layouts, shards(): padded[pool_dest[0]]  43.3 us
    gather x1, local copies, waits for them, and re-layouts, shards(): fine_mid[pool_send[0]]  43.3 us
    gather x4, local copies, waits for them, and re-layouts, graph_layer(): inputs = jnp.concatenate([table[senders], nodes[receivers], edges], axis=1)  34.7 us
    gather x2, local copies, waits for them, and re-layouts, shards(): parents = back.reshape(-1, width)[unpool_slot]  33.5 us
  transfers between devices with their start and end apart: 4, of which 2 were waited for; matrix products, arithmetic and copies ran while one was open for 16% of the time, Pallas kernels for 0%

commit v1 on v0

--- a/solution.py
+++ b/solution.py
@@ -36,7 +36,13 @@
         edge_gain[level],
     )
     partial_sum = jax.ops.segment_sum(message, receivers, num_segments=nodes.shape[0])
-    summed = lax.psum(partial_sum, "edge")
+    parts_n = jax.lax.axis_size("edge")
+    summed = partial_sum
+    for hop_no in [
+        [(w, w ^ nth) for w in range(parts_n)] for nth in (1, 2, 4, 8, 16) if nth < parts_n
+    ]:
+        current_value = jax.lax.ppermute(summed, "edge", hop_no)
+        summed = summed + current_value
     return node_update(
         nodes, summed, node_in_weight[level], node_out_weight[level], node_gain[level]
     )

time: 606 us -> 637 us (1.051)
  waiting for transfers between devices: 74.9 us -> 196 us
  blocking collectives: 103 us -> 0 us
  other arithmetic: 208 us -> 217 us
    ppermute x0 -> x4, waiting for transfers between devices: none -> 122 us  [graph_layer(): current_value = jax.lax.ppermute(summed, 'edge', hop_no)]
    psum x2 -> x0, blocking collectives: 103 us -> none  [graph_layer(): summed = lax.psum(partial_sum, 'edge')]
  transfers between devices with their start and end apart: 4 -> 8, of which waited for: 2 -> 6; matrix products, arithmetic and copies ran while one was open for 16% -> 15% of each run, Pallas kernels for 0% -> 0%
where the time goes in v1:
time: 637 us; the launch traced here: 636 us
  other arithmetic  217 us (34%)
  waiting for transfers between devices  196 us (31%)
  local copies, waits for them, and re-layouts  177 us (28%)
  starting transfers between devices  32 us (5%)
  matrix products  11.5 us (2%)
    ppermute x4, waiting for transfers between devices, graph_layer(): current_value = jax.lax.ppermute(summed, 'edge', hop_no)  122 us
    scatter-add x1, other arithmetic, pooled_mean(): jax.ops.segment_sum(arrived.reshape(-1, width).astype(jnp.float32), place...  76.7 us
    scatter-add x1, other arithmetic, pooled_mean(): jax.ops.segment_sum(jnp.ones_like(places), places, num_segments=COARSE + 1)  75.2 us
    all_to_all x1, waiting for transfers between devices, shards(): lax.all_to_all(padded[pool_dest[0]], 'dom', split_axis=0, concat_axis=0,...  70.3 us
    gather x1, local copies, waits for them, and re-layouts, shards(): fine_mid[pool_send[0]]  43.6 us
    gather x1, local copies, waits for them, and re-layouts, shards(): padded[pool_dest[0]]  43.6 us
    gather x4, local copies, waits for them, and re-layouts, graph_layer(): inputs = jnp.concatenate([table[senders], nodes[receivers], edges], axis=1)  35.7 us
    gather x2, local copies, waits for them, and re-layouts, shards(): parents = back.reshape(-1, width)[unpool_slot]  33.6 us
  transfers between devices with their start and end apart: 8, of which 6 were waited for; matrix products, arithmetic and copies ran while one was open for 15% of the time, Pallas kernels for 0%

profile of v1, /device:TPU:0, one launch (start us, length us, event | category | flops | bytes accessed | tf_op | source)
XLA Modules:
  0.0 635.6 jit_solution(4483356768285883152)
XLA Ops:
  0.6 0.7 compare_select_fusion.8
  1.3 0.1 reshape.183
  1.4 3.5 gather_fusion
  4.9 7.3 %all-to-all-start = ((bf16[8,64,128]{2,1,0:T(8,128)(2,1)}), bf16[8,64,128]{2,1,0:T(8,128)(2,1)S(1)}, u32[]{:S(2)}, u32[]{:S(2)}) async-start(bf16[8,64,128]{2,1,0:T(8,128)(2,1)} %bitcast.1), calls=%async_computation | async-start | bytes 262144 | tf_op jit(solution)/shard_map/all_to_all | solution.py:28
  12.2 0.7 fusion.77
  13.0 0.8 slice_bitcast_fusion.1
  13.7 13.0 %gather_fusion.2 = bf16[4096,128]{1,0:T(8,128)(2,1)S(1)} fusion(bf16[8192,128]{1,0:T(8,128)(2,1)} %param.18, s32[4096]{0:T(1024)S(1)} %fusion.77), kind=kCustom, calls=%fused_computation.2 | custom fusion | bytes 2113536 | tf_op jit(solution)/shard_map/gather | solution.py:30
  26.8 5.5 pad_maximum_fusion
  32.4 16.3 %gather_fusion.1 = bf16[4096,128]{1,0:T(8,128)(2,1)} fusion(bf16[8704,128]{1,0:T(8,128)(2,1)} %pad_maximum_fusion, s32[4096]{0:T(1024)S(1)} %fusion.76), kind=kCustom, calls=%fused_computation.1 | custom fusion | bytes 2113536 | tf_op jit(solution)/shard_map/gather | solution.py:30
  48.7 4.3 fusion.95
  52.9 2.0 multiply_reduce_fusion.1
  54.9 0.2 copy-done.4
  55.2 1.6 multiply_multiply_fusion
  56.8 2.9 copy.25
  59.7 24.8 %scatter_custom_fusion = f32[8192,128]{1,0:T(8,128)} fusion(s32[4096]{0:T(1024)} %param.21, f32[4096,128]{1,0:T(8,128)} %copy.25, f32[]{:T(128)} %constant.13.clone.1), kind=kCustom, calls=%fused_computation.34 | custom fusion | flops 524288 | bytes 4194816 | tf_op jit(solution)/shard_map/scatter-add | solution.py:38
  84.5 7.4 %collective-permute-done = f32[8192,128]{1,0:T(8,128)S(1)} collective-permute-done((f32[8192,128]{1,0:T(8,128)}, f32[8192,128]{1,0:T(8,128)S(1)}, u32[]{:S(2)}, u32[]{:S(2)}) %collective-permute-start) | collective-permute-done | bytes 4194336 | tf_op jit(solution)/shard_map/ppermute | solution.py:44
  91.9 4.7 add.182
  96.6 1.5 collective-permute-start.1
  98.1 2.9 copy.24
  101.0 0.0 copy-start.16
  101.1 88.5 %collective-permute-done.1 = f32[8192,128]{1,0:T(8,128)} collective-permute-done((f32[8192,128]{1,0:T(8,128)}, f32[8192,128]{1,0:T(8,128)}, u32[]{:S(2)}, u32[]{:S(2)}) %collective-permute-start.1) | collective-permute-done | bytes 4194336 | tf_op jit(solution)/shard_map/ppermute | solution.py:44
  189.5 5.2 add_convert_fusion.2
  194.8 5.8 fusion.100
  200.6 2.8 multiply_reduce_fusion
  203.4 0.6 copy-done.2
  204.0 3.8 add_convert_fusion.1
  207.8 3.2 copy.26
  211.0 43.6 %gather_fusion.3 = bf16[12288,128]{1,0:T(8,128)(2,1)} fusion(bf16[8192,128]{1,0:T(8,128)(2,1)S(1)} %copy.26, s32[12288]{0:T(1024)S(1)} %broadcast_clamp_fusion.1), kind=kCustom, calls=%fused_computation.3 | custom fusion | bytes 6340608 | tf_op jit(solution)/shard_map/gather | solution.py:92
  254.6 6.1 all-to-all-start.1
  260.8 0.1 reshape.215
  260.9 75.2 %scatter_custom_fusion.2 = s32[2049]{0:T(1024)S(1)} fusion(s32[12288]{0:T(1024)S(1)} %reshape.263, s32[12288]{0:T(1024)S(1)} %broadcast.163, s32[]{:T(128)} %constant.14.clone.1), kind=kCustom, calls=%fused_computation.103 | custom fusion | flops 12288 | bytes 8200 | tf_op jit(solution)/shard_map/scatter-add | solution.py:55
  336.2 0.0 copy-start.12
  336.2 76.7 %scatter_custom_fusion.1 = f32[2049,128]{1,0:T(8,128)} fusion(s32[12288]{0:T(1024)S(1)} %reshape.263, bf16[12288,128]{1,0:T(8,128)(2,1)S(1)} %bitcast.78, f32[]{:T(128)} %constant.13.clone.1), kind=kCustom, calls=%fused_computation.13 | custom fusion | flops 3145728 | bytes 4194820 | tf_op jit(solution)/shard_map/scatter-add | solution.py:52
  412.9 1.6 fusion.24
  414.5 1.5 gather_fusion.4
  416.0 11.6 %all-to-all-start.2 = ((bf16[8,32,128]{2,1,0:T(8,128)(2,1)}), bf16[8,32,128]{2,1,0:T(8,128)(2,1)S(1)}, u32[]{:S(2)}, u32[]{:S(2)}) async-start(bf16[8,32,128]{2,1,0:T(8,128)(2,1)} %bitcast.13), calls=%async_computation.2 | async-start | bytes 131072 | tf_op jit(solution)/shard_map/all_to_all | solution.py:28
  427.6 3.2 gather_fusion.6
  430.9 0.0 copy-start.14
  430.9 0.0 copy-start.19
  430.9 3.6 all-to-all-done.2
  434.6 3.2 gather_fusion.5
  437.8 0.6 fusion.105
  438.4 0.1 multiply_reduce_fusion.3
  438.5 0.1 multiply_multiply_fusion.1
  438.6 0.2 copy.27
  438.8 6.3 scatter_custom_fusion.3
  445.1 0.1 collective-permute-start.2
  445.2 2.6 collective-permute-done.2
  447.8 0.1 add.199
  447.9 0.0 copy-start.17
  448.0 1.6 collective-permute-start.3
  449.6 23.7 %collective-permute-done.3 = f32[2048,128]{1,0:T(8,128)S(1)} collective-permute-done((f32[2048,128]{1,0:T(8,128)S(1)}, f32[2048,128]{1,0:T(8,128)S(1)}, u32[]{:S(2)}, u32[]{:S(2)}) %collective-permute-start.3) | collective-permute-done | bytes 1048608 | tf_op jit(solution)/shard_map/ppermute | solution.py:44
  473.2 0.1 add_convert_fusion.4
  473.4 0.9 fusion.110
  474.2 0.6 multiply_reduce_fusion.2
  474.9 1.0 add_convert_fusion.3
  475.9 0.8 copy-done.5
  476.7 43.6 %gather_fusion.7 = bf16[12288,128]{1,0:T(8,128)(2,1)} fusion(bf16[2049,128]{1,0:T(8,128)(2,1)S(1)} %concatenate.27, s32[12288]{0:T(1024)S(1)} %broadcast_clamp_fusion), kind=kCustom, calls=%fused_computation.7 | custom fusion | bytes 6340608 | tf_op jit(solution)/shard_map/gather | solution.py:98
  520.3 3.8 all-to-all-start.3
  524.1 70.3 %all-to-all-done.3 = bf16[8,1536,128]{2,1,0:T(8,128)(2,1)S(1)} async-done(((bf16[8,1536,128]{2,1,0:T(8,128)(2,1)}), bf16[8,1536,128]{2,1,0:T(8,128)(2,1)S(1)}, u32[]{:S(2)}, u32[]{:S(2)}) %all-to-all-start.3) | async-done | bytes 3145760 | tf_op jit(solution)/shard_map/all_to_all | solution.py:98
  594.5 29.4 %gather_fusion.8 = bf16[8192,128]{1,0:T(8,128)(2,1)} fusion(bf16[12288,128]{1,0:T(8,128)(2,1)S(1)} %bitcast.77, s32[8192]{0:T(1024)S(1)} %fusion.67), kind=kCustom, calls=%fused_computation.8 | custom fusion | bytes 4227072 | tf_op jit(solution)/shard_map/gather | solution.py:99
  623.9 4.2 copy.28
  628.1 3.4 add_convert_fusion
  631.5 4.1 copy.29
  (66 shorter events, 0.3 us)
Async XLA Ops:
  4.9 21.9 %all-to-all-start = ((bf16[8,64,128]{2,1,0:T(8,128)(2,1)}), bf16[8,64,128]{2,1,0:T(8,128)(2,1)S(1)}, u32[]{:S(2)}, u32[]{:S(2)}) async-start(bf16[8,64,128]{2,1,0:T(8,128)(2,1)} %bitcast.1), calls=%async_computation | async-start | bytes 262144 | tf_op jit(solution)/shard_map/all_to_all | solution.py:28
  13.7 13.0 %copy-start.9 = (s32[4096]{0:T(1024)S(1)}, s32[4096]{0:T(1024)}, u32[]{:S(2)}) copy-start(s32[4096]{0:T(1024)} %param.20) | copy-start | bytes 49156
  13.7 13.1 %copy-start = (bf16[8192,128]{1,0:T(8,128)(2,1)S(1)}, bf16[8192,128]{1,0:T(8,128)(2,1)}, u32[]{:S(2)}) copy-start(bf16[8192,128]{1,0:T(8,128)(2,1)} %param.18) | copy-start | bytes 6291460
  32.4 16.3 %copy-start.15 = (bf16[2,384,128]{2,1,0:T(8,128)(2,1)S(1)}, bf16[2,384,128]{2,1,0:T(8,128)(2,1)}, u32[]{:S(2)}) copy-start(bf16[2,384,128]{2,1,0:T(8,128)(2,1)} %param.30) | copy-start | bytes 589828
  32.4 16.3 %copy-start.18 = (bf16[2,128,128]{2,1,0:T(8,128)(2,1)S(1)}, bf16[2,128,128]{2,1,0:T(8,128)(2,1)}, u32[]{:S(2)}) copy-start(bf16[2,128,128]{2,1,0:T(8,128)(2,1)} %param.31) | copy-start | bytes 196612
  52.9 2.2 copy-start.4
  84.5 7.4 %collective-permute-start = (f32[8192,128]{1,0:T(8,128)}, f32[8192,128]{1,0:T(8,128)S(1)}, u32[]{:S(2)}, u32[]{:S(2)}) collective-permute-start(f32[8192,128]{1,0:T(8,128)} %scatter_custom_fusion), channel_id=1, source_target_pairs={{0,1},{1,0},{2,3},{3,2},{4,5},{5,4},{6,7},{7,6},{8,9},{9,8},{10,11... | collective-permute-start | bytes 12582920 | tf_op jit(solution)/shard_map/ppermute | solution.py:44
  96.6 4.4 copy-start.7
  96.6 4.4 copy-start.13
  96.6 92.9 %collective-permute-start.1 = (f32[8192,128]{1,0:T(8,128)}, f32[8192,128]{1,0:T(8,128)}, u32[]{:S(2)}, u32[]{:S(2)}) collective-permute-start(f32[8192,128]{1,0:T(8,128)} %add.182), channel_id=1, source_target_pairs={{0,2},{1,3},{2,0},{3,1},{4,6},{5,7},{6,4},{7,5},{8,10},{9,11},{10,... | collective-permute-start | bytes 12582920 | tf_op jit(solution)/shard_map/ppermute | solution.py:44
  101.0 93.7 %copy-start.16 = (bf16[2,256,128]{2,1,0:T(8,128)(2,1)S(1)}, bf16[2,256,128]{2,1,0:T(8,128)(2,1)}, u32[]{:S(2)}) copy-start(bf16[2,256,128]{2,1,0:T(8,128)(2,1)} %param.32) | copy-start | bytes 393220
  101.0 93.7 %copy-start.20 = (bf16[2,128,128]{2,1,0:T(8,128)(2,1)S(1)}, bf16[2,128,128]{2,1,0:T(8,128)(2,1)}, u32[]{:S(2)}) copy-start(bf16[2,128,128]{2,1,0:T(8,128)(2,1)} %param.33) | copy-start | bytes 196612
  200.6 3.4 copy-start.2
  254.6 6.2 copy-start.6
  254.6 6.2 copy-start.10
  254.6 81.5 %copy-start.11 = (s32[1024]{0:T(1024)S(1)}, s32[1024]{0:T(1024)}, u32[]{:S(2)}) copy-start(s32[1024]{0:T(1024)} %param.24) | copy-start | bytes 12292
  254.6 81.6 %all-to-all-start.1 = ((bf16[8,1536,128]{2,1,0:T(8,128)(2,1)}), bf16[8,1536,128]{2,1,0:T(8,128)(2,1)S(1)}, u32[]{:S(2)}, u32[]{:S(2)}) async-start(bf16[8,1536,128]{2,1,0:T(8,128)(2,1)} %bitcast.79), calls=%async_computation.1 | async-start | bytes 6291456 | tf_op jit(solution)/shard_map/all_to_all | solution.py:92
  336.2 91.4 %copy-start.12 = (s32[1024]{0:T(1024)S(1)}, s32[1024]{0:T(1024)}, u32[]{:S(2)}) copy-start(s32[1024]{0:T(1024)} %param.25) | copy-start | bytes 12292
  416.0 18.5 %all-to-all-start.2 = ((bf16[8,32,128]{2,1,0:T(8,128)(2,1)}), bf16[8,32,128]{2,1,0:T(8,128)(2,1)S(1)}, u32[]{:S(2)}, u32[]{:S(2)}) async-start(bf16[8,32,128]{2,1,0:T(8,128)(2,1)} %bitcast.13), calls=%async_computation.2 | async-start | bytes 131072 | tf_op jit(solution)/shard_map/all_to_all | solution.py:28
  430.9 6.9 %copy-start.14 = (bf16[1024,128]{1,0:T(8,128)(2,1)S(1)}, bf16[1024,128]{1,0:T(8,128)(2,1)}, u32[]{:S(2)}) copy-start(bf16[1024,128]{1,0:T(8,128)(2,1)} %param.23) | copy-start | bytes 786436
  430.9 6.9 %copy-start.19 = (bf16[2,128,128]{2,1,0:T(8,128)(2,1)S(1)}, bf16[2,128,128]{2,1,0:T(8,128)(2,1)}, u32[]{:S(2)}) copy-start(bf16[2,128,128]{2,1,0:T(8,128)(2,1)} %param.31) | copy-start | bytes 196612
  445.1 2.7 collective-permute-start.2
  447.9 25.4 %copy-start.17 = (bf16[2,256,128]{2,1,0:T(8,128)(2,1)S(1)}, bf16[2,256,128]{2,1,0:T(8,128)(2,1)}, u32[]{:S(2)}) copy-start(bf16[2,256,128]{2,1,0:T(8,128)(2,1)} %param.32) | copy-start | bytes 393220
  448.0 25.4 %copy-start.21 = (bf16[2,128,128]{2,1,0:T(8,128)(2,1)S(1)}, bf16[2,128,128]{2,1,0:T(8,128)(2,1)}, u32[]{:S(2)}) copy-start(bf16[2,128,128]{2,1,0:T(8,128)(2,1)} %param.33) | copy-start | bytes 196612
  448.0 25.3 %collective-permute-start.3 = (f32[2048,128]{1,0:T(8,128)S(1)}, f32[2048,128]{1,0:T(8,128)S(1)}, u32[]{:S(2)}, u32[]{:S(2)}) collective-permute-start(f32[2048,128]{1,0:T(8,128)S(1)} %add.199), channel_id=1, source_target_pairs={{0,2},{1,3},{2,0},{3,1},{4,6},{5,7},{6,4},{7,5},{8,10},{9,11},{10,... | collective-permute-start | bytes 3145736 | tf_op jit(solution)/shard_map/ppermute | solution.py:44
  473.4 1.5 copy-start.3
  475.9 0.8 copy-start.5
  520.3 3.8 copy-start.8
  520.3 74.1 %all-to-all-start.3 = ((bf16[8,1536,128]{2,1,0:T(8,128)(2,1)}), bf16[8,1536,128]{2,1,0:T(8,128)(2,1)S(1)}, u32[]{:S(2)}, u32[]{:S(2)}) async-start(bf16[8,1536,128]{2,1,0:T(8,128)(2,1)} %bitcast.80), calls=%async_computation.3 | async-start | bytes 6291456 | tf_op jit(solution)/shard_map/all_to_all | solution.py:98
  623.9 4.2 copy-start.1
